TPU v7x, 64 devices: a 2x2x8 block of a 4x4x8 slice. The times are simulated.
64 devices in a mesh: dp: 4 (over x, y), tp: 16 (over z, core).
Axes of the slice: x: 2, y: 2, z: 8, core: 2. Of those that a mesh axis runs over, the one named last changes fastest.
The devices are a block of a 4x4x8 slice.
Arguments:
- hidden: bfloat16 [4096, 2048], P('dp'), parts along dimension 0
- tokens: int32 [4096], P('dp'), parts along dimension 0
- embedding: bfloat16 [49152, 2048], P('tp')
- head_w: bfloat16 [2048, 49152], P(None, 'tp')
- h_norm: float32 [2048], replicated
- e_norm: float32 [2048], replicated
- f_norm: float32 [2048], replicated
- o_norm: float32 [2048], replicated
- proj_w: bfloat16 [4096, 2048], P(None, 'tp')
- w_gate: bfloat16 [2048, 8192], P(None, 'tp')
- w_up: bfloat16 [2048, 8192], P(None, 'tp')
- w_down: bfloat16 [8192, 2048], P('tp')
Outputs:
- output 1: bfloat16 [4096, 2048], P('dp'), parts along dimension 0
- output 2: float32 [4096, 49152], P('dp', 'tp'), parts along dimension 0
There are 4 independent parts. A program takes and returns all parts, laid end to end along the dimension named above; an argument that names none is the same for every part.
All inputs are finite; a program needn't handle non-finite values.
Results may differ from a plain program's by a relative error of at most 0.0111877.
Values are sent between devices in bfloat16 or wider.
A program may use at most 768 MiB of HBM per device.

v0:
```python
import jax
import jax.numpy as jnp
from jax import lax
from jax.sharding import PartitionSpec as P

NORM_EPS = 1e-6


def rms_norm(values, norm_gain):
    wide_vals = values.astype(jnp.float32)
    inv_rms = lax.rsqrt(jnp.mean(wide_vals * wide_vals, axis=-1, keepdims=True) + NORM_EPS)
    return wide_vals * inv_rms * norm_gain


def solution(mesh):
    def draft_step(hidden, tokens, embedding, head_w, h_norm, e_norm, f_norm, o_norm, proj_w, w_gate, w_up, w_down):
        tp_index = lax.axis_index("tp")
        vocab_local = embedding.shape[0]
        local_ids = tokens - tp_index * vocab_local
        owned_mask = (local_ids >= 0) & (local_ids < vocab_local)
        picked = jnp.take(embedding, jnp.clip(local_ids, 0, vocab_local - 1), axis=0)
        picked = jnp.where(owned_mask[:, None], picked, jnp.zeros_like(picked))
        emb_rows = lax.psum(picked, "tp")
        joined = jnp.concatenate([rms_norm(hidden, h_norm), rms_norm(emb_rows, e_norm)], axis=-1).astype(jnp.bfloat16)
        proj_cols = jnp.dot(joined, proj_w, preferred_element_type=jnp.float32).astype(jnp.bfloat16)
        proj_full = lax.all_gather(proj_cols, "tp", axis=1, tiled=True)
        normed = rms_norm(proj_full, f_norm).astype(jnp.bfloat16)
        gate_val = jnp.dot(normed, w_gate, preferred_element_type=jnp.float32)
        up_val = jnp.dot(normed, w_up, preferred_element_type=jnp.float32)
        act_val = (jax.nn.silu(gate_val) * up_val).astype(jnp.bfloat16)
        down_part = jnp.dot(act_val, w_down, preferred_element_type=jnp.float32)
        down_sum = lax.psum(down_part, "tp")
        new_u = (proj_full.astype(jnp.float32) + down_sum).astype(jnp.bfloat16)
        out_norm = rms_norm(new_u, o_norm).astype(jnp.bfloat16)
        logits = jnp.dot(out_norm, head_w, preferred_element_type=jnp.float32)
        row_max = lax.pmax(jnp.max(logits, axis=-1), "tp")
        shifted = logits - row_max[:, None]
        row_sum = lax.psum(jnp.sum(jnp.exp(shifted), axis=-1), "tp")
        return new_u, shifted - jnp.log(row_sum)[:, None]

    specs_in = (P("dp", None), P("dp"), P("tp", None), P(None, "tp"), P(None), P(None), P(None), P(None), P(None, "tp"), P(None, "tp"), P(None, "tp"), P("tp", None))
    specs_out = (P("dp", None), P("dp", "tp"))
    return jax.shard_map(draft_step, mesh=mesh, in_specs=specs_in, out_specs=specs_out, check_vma=False)
```

profile of v0, /device:TPU:21, one launch (start us, length us, event | category | flops | bytes accessed | tf_op | source)
XLA Modules:
  0.0 450.0 jit_solution(15457355908834364478)
XLA Ops:
  7.2 0.0 copy-start
  7.2 0.1 all-reduce.3.cloned.1.call-start
  7.3 0.8 compare_and_fusion.1
  8.1 0.7 fusion.31
  8.8 15.0 %gather_fusion = bf16[1024,2048]{1,0:T(8,128)(2,1)} fusion(bf16[3072,2048]{1,0:T(8,128)(2,1)} %param.14, s32[1024]{0:T(1024)S(1)} %fusion.31), kind=kCustom, calls=%fused_computation | custom fusion | bytes 8392704 | tf_op jit(solution)/shard_map/jit(_take)/gather | solution.py:21
  23.8 4.1 select_select_fusion
  27.9 0.0 copy-start.7
  27.9 0.1 all-reduce.3.cloned.1.call-update
  28.0 0.1 all-gather.2.cloned.1.call-start
  28.0 0.0 copy-start.3
  28.0 3.2 fusion
  31.3 0.0 copy-done.7
  31.3 0.2 copy-done.3
  31.5 3.0 fusion.2
  34.5 0.0 copy-start.8
  34.5 112.6 %all-reduce.3.cloned.1.call-done = bf16[1024,2048]{1,0:T(8,128)(2,1)} async-done(((bf16[1024,2048]{1,0:T(8,128)(2,1)}), bf16[1024,2048]{1,0:T(8,128)(2,1)}) %all-reduce.3.cloned.1.call-update) | async-done | bytes 4194320 | tf_op jit(solution)/shard_map/psum | solution.py:23
  147.1 0.0 copy-start.4
  147.1 3.2 fusion.3
  150.4 0.0 copy-done.8
  150.4 0.2 copy-done.4
  150.6 0.0 copy-start.6
  150.6 0.0 copy-start.9
  150.6 1.0 fusion.5
  151.6 1.2 copy-done.6
  152.8 0.3 copy-done.9
  153.1 3.2 fusion.27
  156.2 0.1 all-gather.2.cloned.1.call-update
  156.3 0.2 all-reduce.5.cloned.1.call-start
  156.6 46.1 %all-gather.2.cloned.1.call-done = bf16[1024,2048]{1,0:T(8,128)(2,1)} async-done(((bf16[1024,128]{1,0:T(8,128)(2,1)}), bf16[1024,2048]{1,0:T(8,128)(2,1)}) %all-gather.2.cloned.1.call-update) | async-done | bytes 4194320 | tf_op jit(solution)/shard_map/all_gather | solution.py:26
  202.6 3.2 fusion.9
  205.9 0.0 copy-done.10
  205.9 0.2 copy-done.2
  206.1 5.3 %fusion.22 = f32[1024,512]{1,0:T(8,128)} fusion(bf16[2048,512]{1,0:T(8,128)(2,1)} %param.21, bf16[1024,2048]{1,0:T(8,128)(2,1)S(1)} %copy-done.2, f32[2048]{0:T(1024)S(1)} %copy-done.10, f32[1024]{0:T(1024)S(1)} %add_rsqrt_fusion.1), kind=kOutput, calls=%fused_computation.34 | convolution fusion | flops 2155872256 | bytes 8400896 | tf_op jit(solution)/shard_map/dot_general | solution.py:28
  211.4 0.0 copy-done
  211.4 11.5 %fusion.25 = f32[1024,2048]{1,0:T(8,128)} fusion(bf16[512,2048]{1,0:T(8,128)(2,1)S(1)} %copy-done, f32[1024,512]{1,0:T(8,128)} %fusion.22, bf16[2048,512]{1,0:T(8,128)(2,1)} %param.22, bf16[1024,2048]{1,0:T(8,128)(2,1)} %all-gather.2.cloned.1.call-done, f32[2048]{0:T(1024)S(1)} %copy-done.10, f32[1024]{0:T(1024)S(1)} %add_rsqrt_fusion.1), kind=kOutput, calls=%fused_computation.35 | convolution fusion | flops 4306501632 | bytes 18886656 | tf_op jit(solution)/shard_map/dot_general | solution.py:31
  222.8 0.1 all-reduce.5.cloned.1.call-update
  222.9 0.0 copy-start.11
  222.9 125.6 %all-reduce.5.cloned.1.call-done = f32[1024,2048]{1,0:T(8,128)} async-done(((f32[1024,2048]{1,0:T(8,128)}), f32[1024,2048]{1,0:T(8,128)}) %all-reduce.5.cloned.1.call-update) | async-done | bytes 8388624 | tf_op jit(solution)/shard_map/psum | solution.py:32
  348.5 5.9 %fusion.6 = (f32[1024]{0:T(1024)S(1)}, bf16[1024,2048]{1,0:T(8,128)(2,1)S(1)}) fusion(f32[1024,2048]{1,0:T(8,128)} %all-reduce.5.cloned.1.call-done, bf16[1024,2048]{1,0:T(8,128)(2,1)} %all-gather.2.cloned.1.call-done), kind=kLoop, calls=%fused_computation.18 | loop fusion | flops 12581888 | bytes 16781312 | tf_op jit(solution)/shard_map/reduce_sum | solution.py:11
  354.4 0.0 copy-start.5
  354.4 0.0 copy-done.11
  354.4 19.5 %fusion.35 = (f32[1024]{0:T(1024)S(1)}, f32[1024,3072]{1,0:T(8,128)}) fusion(bf16[2048,3072]{1,0:T(8,128)(2,1)} %param.15, bf16[1024,2048]{1,0:T(8,128)(2,1)S(1)} %get-tuple-element.3, f32[2048]{0:T(1024)S(1)} %copy-done.11, f32[1024]{0:T(1024)S(1)} %add_rsqrt_fusion), kind=kOutput, calls=%fused_computation.48 | convolution fusion | flops 12896435200 | bytes 29376512 | tf_op jit(solution)/shard_map/dot_general | solution.py:35
  373.9 0.0 copy-done.5
  373.9 25.1 %pmax.7 = f32[1024]{0:T(1024)S(1)} all-reduce(f32[1024]{0:T(1024)S(1)} %get-tuple-element.6), channel_id=1, replica_groups=mesh['dp'=4,'tp'=16] {'tp'}, use_global_device_ids=true, to_apply=%region_7.8 | all-reduce | flops 1024 | bytes 8192 | tf_op jit(solution)/shard_map/pmax | solution.py:36
  399.1 6.4 %exponential_reduce_fusion = f32[1024]{0:T(1024)S(1)} fusion(f32[1024,3072]{1,0:T(8,128)} %get-tuple-element.7, f32[1024]{0:T(1024)S(1)} %pmax.7), kind=kLoop, calls=%fused_computation.1 | loop fusion | flops 6290432 | bytes 12591104 | tf_op jit(solution)/shard_map/reduce_sum | solution.py:38
  405.5 25.7 %psum.23 = f32[1024]{0:T(1024)S(1)} all-reduce(f32[1024]{0:T(1024)S(1)} %exponential_reduce_fusion), channel_id=1, replica_groups=mesh['dp'=4,'tp'=16] {'tp'}, use_global_device_ids=true, to_apply=%region_9.10 | all-reduce | flops 1024 | bytes 8192 | tf_op jit(solution)/shard_map/psum | solution.py:38
  431.2 12.2 %subtract_subtract_fusion = f32[1024,3072]{1,0:T(8,128)} fusion(f32[1024,3072]{1,0:T(8,128)} %get-tuple-element.7, f32[1024]{0:T(1024)S(1)} %log.3, f32[1024]{0:T(1024)S(1)} %pmax.7), kind=kLoop, calls=%fused_computation.5 | loop fusion | flops 6291456 | bytes 25174016 | tf_op jit(solution)/shard_map/sub | solution.py:39
  443.4 0.0 copy-done.1
  (8 shorter events, 0.0 us)
Async XLA Ops:
  7.2 204.2 %copy-start = (bf16[512,2048]{1,0:T(8,128)(2,1)S(1)}, bf16[512,2048]{1,0:T(8,128)(2,1)}, u32[]{:S(2)}) copy-start(bf16[512,2048]{1,0:T(8,128)(2,1)} %param.23) | copy-start | bytes 6291460
  7.2 139.9 %all-reduce.3.cloned.1.call-start = ((), (), s32[]{:S(2)}) async-start(), calls=%async_computation | async-start | bytes 8388608 | tf_op jit(solution)/shard_map/psum | solution.py:23
  27.9 3.4 copy-start.7
  28.0 174.7 %all-gather.2.cloned.1.call-start = ((), (), s32[]{:S(2)}) async-start(), calls=%async_computation.1 | async-start | bytes 4456448 | tf_op jit(solution)/shard_map/all_gather | solution.py:26
  28.0 3.5 copy-start.3
  34.5 115.8 %copy-start.8 = (f32[2048]{0:T(1024)S(1)}, f32[2048]{0:T(1024)}, u32[]{:S(2)}) copy-start(f32[2048]{0:T(1024)} %param.17) | copy-start | bytes 24580
  147.1 3.4 copy-start.4
  150.6 2.2 copy-start.6
  150.6 2.5 copy-start.9
  156.2 49.6 %copy-start.10 = (f32[2048]{0:T(1024)S(1)}, f32[2048]{0:T(1024)}, u32[]{:S(2)}) copy-start(f32[2048]{0:T(1024)} %param.18) | copy-start | bytes 24580
  156.3 192.2 %all-reduce.5.cloned.1.call-start = ((), (), s32[]{:S(2)}) async-start(), calls=%async_computation.2 | async-start | bytes 16777216 | tf_op jit(solution)/shard_map/psum | solution.py:32
  202.6 3.4 copy-start.2
  222.9 131.5 %copy-start.11 = (f32[2048]{0:T(1024)S(1)}, f32[2048]{0:T(1024)}, u32[]{:S(2)}) copy-start(f32[2048]{0:T(1024)} %param.19) | copy-start | bytes 24580
  354.4 19.5 %copy-start.5 = (bf16[1024,2048]{1,0:T(8,128)(2,1)}, bf16[1024,2048]{1,0:T(8,128)(2,1)S(1)}, u32[]{:S(2)}) copy-start(bf16[1024,2048]{1,0:T(8,128)(2,1)S(1)} %get-tuple-element.3) | copy-start | bytes 12582916
  431.2 12.2 %copy-start.1 = (bf16[512,2048]{1,0:T(8,128)(2,1)S(1)}, bf16[512,2048]{1,0:T(8,128)(2,1)}, u32[]{:S(2)}) copy-start(bf16[512,2048]{1,0:T(8,128)(2,1)} %param.23) | copy-start | bytes 6291460
Sparse Core Ops, SparseCore 0:
  28.1 119.0 all-reduce.2
  156.4 46.1 all-gather.1
  223.0 125.4 all-reduce.4
where the time goes:
time: 450 us
  waiting for transfers between devices  284 us (63%)
  blocking collectives  50.9 us (11%)
  other arithmetic  43.8 us (10%)
  matrix products  39.4 us (9%)
  local copies, waits for them, and re-layouts  17.1 us (4%)
  between operations  13.9 us (3%)
    psum x1, waiting for transfers between devices, draft_step(): down_sum = lax.psum(down_part, 'tp')  126 us
    psum x1, waiting for transfers between devices, draft_step(): emb_rows = lax.psum(picked, 'tp')  113 us
    all_gather x1, waiting for transfers between devices, draft_step(): proj_full = lax.all_gather(proj_cols, 'tp', axis=1, tiled=True)  46.1 us
    psum x1, blocking collectives, draft_step(): row_sum = lax.psum(jnp.sum(jnp.exp(shifted), axis=-1), 'tp')  25.7 us
    pmax x1, blocking collectives, draft_step(): row_max = lax.pmax(jnp.max(logits, axis=-1), 'tp')  25.1 us
    dot_general x1, matrix products, draft_step(): logits = jnp.dot(out_norm, head_w, preferred_element_type=jnp.float32)  19.5 us
    reduce_sum x4, other arithmetic, rms_norm(): jnp.mean(wide_vals * wide_vals, axis=-1, keepdims=True) + NORM_EPS  15.5 us
    gather x1, local copies, waits for them, and re-layouts, draft_step(): jnp.take(embedding, jnp.clip(local_ids, 0, vocab_local - 1), axis=0)  15 us
  transfers between devices with their start and end apart: 3, of which 3 were waited for; matrix products, arithmetic and copies ran while one was open for 1% of the time, Pallas kernels for 0%

commit v1 on v0

v1 whole, which is shorter than its diff:
```python
import functools

import jax
import jax.numpy as jnp
from jax import lax
from jax.experimental import pallas as pl
from jax.experimental.pallas import tpu as pltpu
from jax.sharding import PartitionSpec as P

NORM_EPS = 1e-6
BF16 = jnp.bfloat16
F32 = jnp.float32
GROUP_ROWS = 256
CORES = 2
SEND_R, SEND_L, FROM_L, FROM_R = range(4)
E_RS, E_AG, P_AG, D_RS, U_AG = range(5)


def norm_rows(values, gain):
    wide = values.astype(F32)
    inv = lax.rsqrt(jnp.mean(wide * wide, axis=-1, keepdims=True) + NORM_EPS)
    return wide * inv * gain


def aligned(index, size):
    return pl.ds(pl.multiple_of(index * size, size), size)


def tile_of(width, most):
    return min(width, most)


def step_kernel(
    n_tp, tok, hg, eg, fg, og, hid_h, emb_h, head_h, pw_h, wg_h, wu_h, wd_h,
    u_h, z_h, lse,
    big, hid, pu, land, ebuf, pbuf, part, pw, wg, wu, wd, erl, err, drl, drr,
    onehot, nbuf, abuf, obuf, zst, mst, sst, stats,
    ring, xsend, xrecv, wsend, wrecv, ssend, srecv, lsem, bsem, hsem, zsem, usem,
):
    groups, half_rows, dim = hid.shape
    chips = n_tp // CORES
    hops = chips // 2
    rows = CORES * half_rows
    blk = half_rows // chips
    hcol = dim // 2
    hrow = half_rows // 2
    pcols = pw.shape[1] // CORES
    fcols = wg.shape[1] // CORES
    vocab = zst.shape[1]
    q = big.shape[1]
    n_vq, n_dq = vocab // q, dim // q

    me = lax.axis_index("tp")
    z, k = me // CORES, lax.rem(me, CORES)
    other = 1 - k
    sib = z * CORES + other
    right = lax.rem(me + CORES, n_tp)
    left = lax.rem(me + n_tp - CORES, n_tp)

    def chip(offset):
        return lax.rem(z + offset + chips, chips)

    def remote(src, dst, ssem, rsem, dev):
        return pltpu.make_async_remote_copy(
            src_ref=src, dst_ref=dst, send_sem=ssem, recv_sem=rsem,
            device_id={"tp": dev}, device_id_type=pl.DeviceIdType.MESH,
        )

    def emb_copy(i, j):
        return pltpu.make_async_copy(
            emb_h.at[pl.ds(i * q, q), pl.ds(j * q, q)], big.at[i * n_dq + j], bsem.at[i * n_dq + j])

    def head_copy(i, j):
        return pltpu.make_async_copy(
            head_h.at[pl.ds(i * q, q), pl.ds(j * q, q)], big.at[i * n_vq + j], hsem.at[i * n_vq + j])

    def hid_copy(g):
        return pltpu.make_async_copy(
            hid_h.at[pl.ds(pl.multiple_of(g * rows + k * half_rows, half_rows), half_rows)], hid.at[g], lsem.at[4 + g])

    own_pw = pw.at[:, aligned(k, pcols)]
    own_wg = wg.at[:, aligned(k, fcols)]
    own_wu = wu.at[:, aligned(k, fcols)]
    own_wd = wd.at[aligned(k, fcols), :]
    oth_pw = pw.at[:, aligned(other, pcols)]
    oth_wg = wg.at[:, aligned(other, fcols)]
    oth_wu = wu.at[:, aligned(other, fcols)]
    oth_wd = wd.at[aligned(other, fcols), :]
    w_local = [pltpu.make_async_copy(s, d, lsem.at[i]) for i, (s, d) in enumerate(
        [(pw_h, own_pw), (wg_h, own_wg), (wu_h, own_wu), (wd_h, own_wd)])]
    w_send = [remote(r, r, wsend.at[i], wrecv.at[i], sib) for i, r in enumerate([own_pw, own_wg, own_wu, own_wd])]
    w_recv = [remote(r, r, wsend.at[i], wrecv.at[i], sib) for i, r in enumerate([oth_pw, oth_wg, oth_wu, oth_wd])]

    for i in range(n_vq):
        for j in range(n_dq):
            emb_copy(i, j).start()
    for c in w_local:
        c.start()

    @pl.loop(0, groups)
    def _(g):
        hid_copy(g).start()

    barrier = pltpu.get_barrier_semaphore()
    for d in range(1, n_tp):
        pl.semaphore_signal(barrier, inc=1, device_id={"tp": lax.rem(me + d, n_tp)}, device_id_type=pl.DeviceIdType.MESH)
    pl.semaphore_wait(barrier, n_tp - 1)

    def e_blk(g, o, h):
        cols = pl.ds(0, dim) if h is None else pl.ds(h * hcol, hcol)
        return ebuf.at[g, aligned(o, blk), cols]

    def p_blk(g, o, h):
        r = pl.ds(0, half_rows) if h is None else pl.ds(h * hrow, hrow)
        return pbuf.at[g, r, aligned(o, CORES * pcols)]

    def u_blk(g, o, h):
        cols = pl.ds(0, dim) if h is None else pl.ds(h * hcol, hcol)
        return pu.at[g, pl.ds(pl.multiple_of(k * half_rows + o * blk, blk), blk), cols]

    def ag_pair(c, block, g, s):
        last = s == hops
        r = block(g, chip(-(s - 1)), 0 if last else None)
        l = block(g, chip(s - 1), 1 if last else None)
        return (remote(r, r, ring.at[c, SEND_R, g, s - 1], ring.at[c, FROM_L, g, s - 1], right),
                remote(l, l, ring.at[c, SEND_L, g, s - 1], ring.at[c, FROM_R, g, s - 1], left))

    def ag_wait(c, block, g, s):
        last = s == hops
        r = block(g, chip(-s), 0 if last else None)
        l = block(g, chip(s), 1 if last else None)
        return (remote(r, r, ring.at[c, SEND_R, g, s - 1], ring.at[c, FROM_L, g, s - 1], right),
                remote(l, l, ring.at[c, SEND_L, g, s - 1], ring.at[c, FROM_R, g, s - 1], left))

    def ag_send(c, block, g, s):
        for cp in ag_pair(c, block, g, s):
            cp.start()

    def ag_step(c, block, g, s):
        got, send = ag_wait(c, block, g, s - 1), ag_pair(c, block, g, s)
        for a, b in zip(got, send):
            a.wait_recv()
            b.start()

    def rs_part(ref, h):
        return ref if h is None else ref.at[:, pl.ds(h * hcol, hcol)]

    def rs_pair(c, own, lands, g, s):
        out = []
        for kind, frm, side, dev, h1, sign in ((SEND_R, FROM_L, 0, right, 0, 1), (SEND_L, FROM_R, 1, left, 1, -1)):
            h = h1 if s == 1 else None
            dst = rs_part(lands[side].at[g, s - 1], h)
            src = rs_part(own.at[g, aligned(chip(sign * hops), blk)], h) if s == 1 else lands[side].at[g, s - 2]
            out.append(remote(src, dst, ring.at[c, kind, g, s - 1], ring.at[c, frm, g, s - 1], dev))
        return out

    def rs_wait(c, own, lands, g, s):
        return rs_pair(c, own, lands, g, s)

    def rs_first(c, own, lands, g):
        for cp in rs_pair(c, own, lands, g, 1):
            cp.start()

    def rs_step(c, own, lands, g, s):
        got, send = rs_wait(c, own, lands, g, s - 1), rs_pair(c, own, lands, g, s)
        for side, sign in ((0, 1), (1, -1)):
            got[side].wait_recv()
            o = aligned(chip(sign * (hops + 1 - s)), blk)
            slot = lands[side].at[g, s - 2]
            if s == 2:
                for h in range(2):
                    c_ = slice(h * hcol, (h + 1) * hcol)
                    mine = own[g, o, c_]
                    slot[:, c_] = slot[:, c_] + mine if h == side else mine
            else:
                slot[...] = slot[...] + own[g, o, :]
            send[side].start()

    def rs_sum(c, own, lands, g):
        for cp in rs_wait(c, own, lands, g, hops):
            cp.wait_recv()
        mine = own[g, aligned(z, blk), :]
        return lands[0][g, hops - 1].astype(F32) + mine.astype(F32) + lands[1][g, hops - 1].astype(F32)

    e_lands, d_lands = (erl, err), (drl, drr)

    def pick_swap(g):
        return remote(pu.at[g, aligned(other, half_rows)], land.at[g], xsend.at[0, g], xrecv.at[0, g], sib)

    def u_swap(g, c):
        r = pu.at[g, aligned(c, half_rows)]
        return remote(r, r, xsend.at[1, g], xrecv.at[1, g], sib)

    def stat_send(g, d):
        return remote(stats.at[g, me], stats.at[g, me], ssend.at[g, d], srecv.at[g, d], lax.rem(me + d, n_tp))

    def stat_wait(g, d):
        src = lax.rem(me + n_tp - d, n_tp)
        return remote(stats.at[g, src], stats.at[g, src], ssend.at[g, d], srecv.at[g, d], lax.rem(me + d, n_tp))

    def z_copy(g, j):
        return pltpu.make_async_copy(
            zst.at[:, pl.ds(j * q, q)], z_h.at[aligned(g, rows), pl.ds(j * q, q)], zsem.at[j])

    def u_copy(g):
        return pltpu.make_async_copy(pu.at[g], u_h.at[aligned(g, rows)], usem.at[g])

    def picks(g):
        @pl.when(g == 0)
        def _():
            for i in range(n_vq):
                for j in range(n_dq):
                    emb_copy(i, j).wait()

        ids = tok[aligned(g, rows), :] - me * vocab
        lanes = ids.shape[1]
        lane = lax.broadcasted_iota(jnp.int32, ids.shape, 1)

        @pl.loop(0, vocab // lanes)
        def _(j):
            onehot[:, aligned(j, lanes)] = jnp.where(ids - j * lanes == lane, 1.0, 0.0).astype(BF16)

        tn = tile_of(q, 512)
        for j in range(n_dq):
            @pl.loop(0, q // tn)
            def _(t):
                acc = None
                for i in range(n_vq):
                    d = jnp.dot(onehot[:, i * q:(i + 1) * q], big[i * n_dq + j, :, aligned(t, tn)], preferred_element_type=F32)
                    acc = d if acc is None else acc + d
                pu[g, :, pl.ds(pl.multiple_of(j * q + t * tn, tn), tn)] = acc.astype(BF16)

        pick_swap(g).start()

        @pl.when(g == groups - 1)
        def _():
            for i in range(n_dq):
                for j in range(n_vq):
                    head_copy(i, j).start()

        @pl.when(g == 0)
        def _():
            w_local[0].wait()
            w_send[0].start()

    def pick_sum(g):
        pick_swap(g).wait_recv()

        @pl.loop(0, chips)
        def _(i):
            r = aligned(i, blk)
            land[g, r, :] = land[g, r, :] + pu[g, pl.ds(pl.multiple_of(k * half_rows + i * blk, blk), blk), :]

        rs_first(E_RS, land, e_lands, g)

    def e_norm(g):
        pick_swap(g).wait_send()
        ebuf[g, aligned(z, blk), :] = norm_rows(rs_sum(E_RS, land, e_lands, g), eg[...]).astype(BF16)
        ag_send(E_AG, e_blk, g, 1)

    def h_norm(g):
        hid_copy(g).wait()

        @pl.loop(0, chips)
        def _(i):
            r = aligned(i, blk)
            hid[g, r, :] = norm_rows(hid[g, r, :], hg[...]).astype(BF16)

        @pl.when(g == 0)
        def _():
            for i in range(1, 4):
                w_local[i].wait()
                w_send[i].start()

    def project(g):
        for cp in ag_wait(E_AG, e_blk, g, hops):
            cp.wait_recv()

        @pl.when(g == 0)
        def _():
            w_recv[0].wait_recv()

        out = jnp.dot(hid[g], pw[:dim, :], preferred_element_type=F32)
        out += jnp.dot(ebuf[g], pw[dim:, :], preferred_element_type=F32)
        pbuf[g, :, aligned(z, CORES * pcols)] = out.astype(BF16)
        ag_send(P_AG, p_blk, g, 1)

    def feed_forward(g):
        for cp in ag_wait(P_AG, p_blk, g, hops):
            cp.wait_recv()

        @pl.when(g == 0)
        def _():
            for i in range(1, 4):
                w_recv[i].wait_recv()

        @pl.loop(0, chips)
        def _(i):
            r = aligned(i, blk)
            nbuf[r, :] = norm_rows(pbuf[g, r, :], fg[...]).astype(BF16)

        width = wg.shape[1]
        tn = tile_of(width, 256)

        @pl.loop(0, width // tn)
        def _(t):
            c = aligned(t, tn)
            gate = jnp.dot(nbuf[...], wg[:, c], preferred_element_type=F32)
            up = jnp.dot(nbuf[...], wu[:, c], preferred_element_type=F32)
            abuf[:, c] = (jax.nn.silu(gate) * up).astype(BF16)

        tm = tile_of(dim, 512)

        @pl.loop(0, dim // tm)
        def _(t):
            c = aligned(t, tm)
            part[g, :, c] = jnp.dot(abuf[...], wd[:, c], preferred_element_type=F32)

        rs_first(D_RS, part, d_lands, g)

    def new_u(g):
        total = rs_sum(D_RS, part, d_lands, g)
        total = pbuf[g, aligned(z, blk), :].astype(F32) + total
        pu[g, pl.ds(pl.multiple_of(k * half_rows + z * blk, blk), blk), :] = total.astype(BF16)
        ag_send(U_AG, u_blk, g, 1)

    def u_done(g):
        for cp in ag_wait(U_AG, u_blk, g, hops):
            cp.wait_recv()
        u_swap(g, k).start()

    def head(g):
        u_swap(g, other).wait_recv()
        u_copy(g).start()

        @pl.when(g == 0)
        def _():
            for i in range(n_dq):
                for j in range(n_vq):
                    head_copy(i, j).wait()

        @pl.loop(0, rows // blk)
        def _(i):
            r = aligned(i, blk)
            obuf[r, :] = norm_rows(pu[g, r, :], og[...]).astype(BF16)

        tn = tile_of(q, 512)
        for j in range(n_vq):
            @pl.when(g > 0)
            def _():
                z_copy(g - 1, j).wait()

            @pl.loop(0, q // tn)
            def _(t):
                acc = None
                for i in range(n_dq):
                    d = jnp.dot(obuf[:, i * q:(i + 1) * q], big[i * n_vq + j, :, aligned(t, tn)], preferred_element_type=F32)
                    acc = d if acc is None else acc + d
                zst[:, pl.ds(pl.multiple_of(j * q + t * tn, tn), tn)] = acc

            z_copy(g, j).start()

        @pl.loop(0, rows // blk)
        def _(i):
            r = aligned(i, blk)
            zz = zst[r, :]
            m = jnp.max(zz, axis=-1, keepdims=True)
            s = jnp.sum(jnp.exp(zz - m), axis=-1, keepdims=True)
            mst[r, :] = jnp.broadcast_to(m, (blk, mst.shape[1]))
            sst[r, :] = jnp.broadcast_to(s, (blk, sst.shape[1]))

        mt, st = mst[...].T, sst[...].T
        lanes = stats.shape[3]
        n = rows // lanes
        for i in range(n):
            c = slice(i * lanes, (i + 1) * lanes)
            stats[g, me, i:i + 1, :] = mt[0:1, c]
            stats[g, me, n + i:n + i + 1, :] = st[0:1, c]
        for d in range(1, n_tp):
            stat_send(g, d).start()

    def total_lse(g):
        for d in range(1, n_tp):
            stat_wait(g, d).wait_recv()
        n = rows // stats.shape[3]
        ms = [stats[g, i, 0:n, :] for i in range(n_tp)]
        top = functools.reduce(jnp.maximum, ms)
        tot = functools.reduce(jnp.add, [stats[g, i, n:2 * n, :] * jnp.exp(ms[i] - top) for i in range(n_tp)])
        lse[g, 0:n, :] = top + jnp.log(tot)

    stages = [picks, pick_sum]
    stages += [functools.partial(rs_step, E_RS, land, e_lands, s=s) for s in range(2, hops + 1)]
    stages += [e_norm]
    stages += [functools.partial(ag_step, E_AG, e_blk, s=s) for s in range(2, hops + 1)]
    h_at = len(stages) - 1
    stages += [project]
    stages += [functools.partial(ag_step, P_AG, p_blk, s=s) for s in range(2, hops + 1)]
    stages += [feed_forward]
    stages += [functools.partial(rs_step, D_RS, part, d_lands, s=s) for s in range(2, hops + 1)]
    stages += [new_u]
    stages += [functools.partial(ag_step, U_AG, u_blk, s=s) for s in range(2, hops + 1)]
    stages += [u_done]
    head_at = len(stages)
    stages += [head, total_lse]
    order = [i for i in range(len(stages) - 1, -1, -1) if i not in (head_at,)] + [head_at]

    @pl.loop(0, groups + len(stages) - 1)
    def _(t):
        for i in order:
            g = t - i

            @pl.when((g >= 0) & (g < groups))
            def _():
                stages[i](g=g)
                if i == h_at:
                    h_norm(g)

    for cp in w_send:
        cp.wait_send()
    for j in range(n_vq):
        z_copy(groups - 1, j).wait()

    @pl.loop(0, groups)
    def _(g):
        for s in range(1, hops + 1):
            for cp in rs_pair(E_RS, land, e_lands, g, s) + rs_pair(D_RS, part, d_lands, g, s):
                cp.wait_send()
            for c, b in ((E_AG, e_blk), (P_AG, p_blk), (U_AG, u_blk)):
                for cp in ag_pair(c, b, g, s):
                    cp.wait_send()
        u_swap(g, k).wait_send()
        for d in range(1, n_tp):
            stat_send(g, d).wait_send()
        u_copy(g).wait()


def draft_call(n_tp, hidden, tokens, embedding, head_w, h_norm, e_norm, f_norm, o_norm, proj_w, w_gate, w_up, w_down):
    batch, dim = hidden.shape
    vocab = embedding.shape[0]
    pcols, fcols = proj_w.shape[1], w_gate.shape[1]
    groups = batch // GROUP_ROWS
    half_rows = GROUP_ROWS // CORES
    chips = n_tp // CORES
    hops = chips // 2
    blk = half_rows // chips
    q = dim // 2
    lanes = 128
    tok = jnp.broadcast_to(tokens[:, None], (batch, lanes))
    vm = pl.BlockSpec(memory_space=pltpu.VMEM)
    anyspec = pl.BlockSpec(memory_space=pl.ANY)
    dma = pltpu.SemaphoreType.DMA
    n_big = (vocab // q) * (dim // q)
    flops = 2 * batch * (2 * dim * vocab + 2 * dim * pcols + 3 * dim * fcols)
    return pl.pallas_call(
        functools.partial(step_kernel, n_tp),
        out_shape=(
            jax.ShapeDtypeStruct((batch, dim), BF16),
            jax.ShapeDtypeStruct((batch, vocab), F32),
            jax.ShapeDtypeStruct((groups, 8, lanes), F32),
        ),
        in_specs=[vm] * 5 + [anyspec] * 7,
        out_specs=(anyspec, anyspec, vm),
        scratch_shapes=[
            pltpu.VMEM((n_big, q, q), BF16),
            pltpu.VMEM((groups, half_rows, dim), BF16),
            pltpu.VMEM((groups, GROUP_ROWS, dim), BF16),
            pltpu.VMEM((groups, half_rows, dim), BF16),
            pltpu.VMEM((groups, half_rows, dim), BF16),
            pltpu.VMEM((groups, half_rows, dim), BF16),
            pltpu.VMEM((groups, half_rows, dim), F32),
            pltpu.VMEM((2 * dim, CORES * pcols), BF16),
            pltpu.VMEM((dim, CORES * fcols), BF16),
            pltpu.VMEM((dim, CORES * fcols), BF16),
            pltpu.VMEM((CORES * fcols, dim), BF16),
            pltpu.VMEM((groups, hops, blk, dim), BF16),
            pltpu.VMEM((groups, hops, blk, dim), BF16),
            pltpu.VMEM((groups, hops, blk, dim), F32),
            pltpu.VMEM((groups, hops, blk, dim), F32),
            pltpu.VMEM((GROUP_ROWS, vocab), BF16),
            pltpu.VMEM((half_rows, dim), BF16),
            pltpu.VMEM((half_rows, CORES * fcols), BF16),
            pltpu.VMEM((GROUP_ROWS, dim), BF16),
            pltpu.VMEM((GROUP_ROWS, vocab), F32),
            pltpu.VMEM((GROUP_ROWS, lanes), F32),
            pltpu.VMEM((GROUP_ROWS, lanes), F32),
            pltpu.VMEM((groups, n_tp, 8, lanes), F32),
            dma((5, 4, groups, hops)),
            dma((2, groups)),
            dma((2, groups)),
            dma((4,)),
            dma((4,)),
            dma((groups, n_tp)),
            dma((groups, n_tp)),
            dma((4 + groups,)),
            dma((n_big,)),
            dma((n_big,)),
            dma((vocab // q,)),
            dma((groups,)),
        ],
        compiler_params=pltpu.CompilerParams(
            collective_id=0, has_side_effects=True, vmem_limit_bytes=67043328),
        cost_estimate=pl.CostEstimate(flops=flops, bytes_accessed=70 << 20, transcendentals=0),
        name="draft_step",
    )(tok, h_norm[None], e_norm[None], f_norm[None], o_norm[None], hidden, embedding, head_w, proj_w, w_gate, w_up, w_down)


def solution(mesh):
    n_tp = mesh.shape["tp"]

    def draft_step(hidden, *rest):
        new_u, logits, lse = draft_call(n_tp, hidden, *rest)
        groups = lse.shape[0]
        lse_rows = lse[:, : GROUP_ROWS // lse.shape[2], :].reshape(hidden.shape[0])
        return new_u, logits - lse_rows[:, None]

    specs_in = (P("dp", None), P("dp"), P("tp", None), P(None, "tp"), P(None), P(None), P(None), P(None), P(None, "tp"), P(None, "tp"), P(None, "tp"), P("tp", None))
    specs_out = (P("dp", None), P("dp", "tp"))
    return jax.shard_map(draft_step, mesh=mesh, in_specs=specs_in, out_specs=specs_out, check_vma=False)
```

time: 450 us -> 235 us (0.52)
  waiting for transfers between devices: 284 us -> 0 us
  Pallas kernels: 0 us -> 217 us
  blocking collectives: 50.9 us -> 0 us
  matrix products: 39.4 us -> 0 us
  other arithmetic: 43.8 us -> 12 us
  between operations: 13.9 us -> 0.64 us
  local copies, waits for them, and re-layouts: 17.1 us -> 4.42 us
    psum x2 -> x0, waiting for transfers between devices: 238 us -> none  [the longest x1 126 us: draft_step(): down_sum = lax.psum(down_part, 'tp')]
    pallas_call x0 -> x1, Pallas kernels: none -> 217 us  [draft_call(): pl.pallas_call(functools.partial(step_kernel, n_tp), out_shape=(jax.Shape...]
    all_gather x1 -> x0, waiting for transfers between devices: 46.1 us -> none  [draft_step(): proj_full = lax.all_gather(proj_cols, 'tp', axis=1, tiled=True)]
    dot_general x4 -> x0, matrix products: 39.4 us -> none  [the longest x1 19.5 us: draft_step(): logits = jnp.dot(out_norm, head_w, preferred_element_type=jnp.float32)]
    psum x1 -> x0, blocking collectives: 25.7 us -> none  [draft_step(): row_sum = lax.psum(jnp.sum(jnp.exp(shifted), axis=-1), 'tp')]
    pmax x1 -> x0, blocking collectives: 25.1 us -> none  [draft_step(): row_max = lax.pmax(jnp.max(logits, axis=-1), 'tp')]
    reduce_sum x5 -> x0, other arithmetic: 21.9 us -> none  [the longest x4 15.5 us: rms_norm(): jnp.mean(wide_vals * wide_vals, axis=-1, keepdims=True) + NORM_EPS]
    gather x1 -> x0, local copies, waits for them, and re-layouts: 15 us -> none  [draft_step(): jnp.take(embedding, jnp.clip(local_ids, 0, vocab_local - 1), axis=0)]
  transfers between devices with their start and end apart: 3 -> 0, of which waited for: 3 -> 0; matrix products, arithmetic and copies ran while one was open for 1% -> 0% of each run, Pallas kernels for 0% -> 0%
where the time goes in v1:
time: 235 us; the launch traced here: 234 us
  Pallas kernels  217 us (92%)
  other arithmetic  12 us (5%)
  local copies, waits for them, and re-layouts  4.42 us (2%)
    pallas_call x1, Pallas kernels, draft_call(): pl.pallas_call(functools.partial(step_kernel, n_tp), out_shape=(jax.Shape...  217 us
    sub x1, other arithmetic, draft_step(): return (new_u, logits - lse_rows[:, None])  12 us

profile of v1, /device:TPU:21, one launch (start us, length us, event | category | flops | bytes accessed | tf_op | source)
XLA Modules:
  0.0 234.5 jit_solution(4377411851416789011)
XLA Ops:
  0.6 1.7 broadcast_in_dim.18.tok
  2.3 217.4 %draft_step.1 = (bf16[1024,2048]{1,0:T(8,128)(2,1)}, f32[1024,3072]{1,0:T(8,128)}, f32[4,8,128]{2,1,0:T(8,128)}) custom-call(s32[1024,128]{1,0:T(8,128)} %broadcast_in_dim.18.tok, f32[1,2048]{1,0:T(1,128)} %bitcast.6, f32[1,2048]{1,0:T(1,128)} %bitcast.7, f32[1,2048]{1,0:T(1,128)} %bitcast.8, f32[1,2048]{1,0:T(1,128)} %bitcast.9, bf16[1024,2048]{1,0:T(8,128)(2,1)} %hid_h.1, ...), custom_call_target="tpu_custom_call" | custom-call | flops 33285996544 | bytes 73400320 | tf_op jit(solution)/shard_map/draft_step/pallas_call | solution.py:454
  219.7 0.7 slice.3
  220.4 0.0 copy-start
  220.5 12.0 %broadcast_subtract_fusion = f32[1024,3072]{1,0:T(8,128)} fusion(f32[1024,3072]{1,0:T(8,128)} %get-tuple-element.6, f32[1024]{0:T(1024)S(1)} %bitcast.5), kind=kLoop, calls=%fused_computation | loop fusion | flops 3145728 | bytes 25169920 | tf_op jit(solution)/shard_map/sub | solution.py:514
  232.5 0.0 copy-done
  232.5 2.0 copy.15
Async XLA Ops:
  220.4 12.0 %copy-start = (bf16[1024,2048]{1,0:T(8,128)(2,1)S(1)}, bf16[1024,2048]{1,0:T(8,128)(2,1)}, u32[]{:S(2)}) copy-start(bf16[1024,2048]{1,0:T(8,128)(2,1)} %get-tuple-element.10) | copy-start | bytes 12582916

commit v2 on v1

--- a/solution.py
+++ b/solution.py
@@ -11,6 +11,7 @@
 BF16 = jnp.bfloat16
 F32 = jnp.float32
 GROUP_ROWS = 256
+KERNEL_VMEM = 46 << 20
 CORES = 2
 SEND_R, SEND_L, FROM_L, FROM_R = range(4)
 E_RS, E_AG, P_AG, D_RS, U_AG = range(5)
@@ -22,6 +23,24 @@
     return wide * inv * gain
 
 
+def norm_into(load, store, gain, n_rows, unit=16, width=4):
+    width = min(width, n_rows // unit)
+
+    @pl.loop(0, n_rows // (unit * width))
+    def _(i):
+        rows = [pl.ds(pl.multiple_of((i * width + u) * unit, unit), unit) for u in range(width)]
+        scales = []
+        for r in rows:
+            wide = load(r).astype(F32)
+            scales.append(lax.rsqrt(jnp.mean(wide * wide, axis=-1, keepdims=True) + NORM_EPS))
+        for r, inv in zip(rows, scales):
+            store(r, (load(r).astype(F32) * inv * gain[...]).astype(BF16))
+
+
+def columns_of(row, lanes):
+    return jnp.broadcast_to(row, (lanes, lanes)).T
+
+
 def aligned(index, size):
     return pl.ds(pl.multiple_of(index * size, size), size)
 
@@ -32,10 +51,10 @@
 
 def step_kernel(
     n_tp, tok, hg, eg, fg, og, hid_h, emb_h, head_h, pw_h, wg_h, wu_h, wd_h,
-    u_h, z_h, lse,
-    big, hid, pu, land, ebuf, pbuf, part, pw, wg, wu, wd, erl, err, drl, drr,
-    onehot, nbuf, abuf, obuf, zst, mst, sst, stats,
-    ring, xsend, xrecv, wsend, wrecv, ssend, srecv, lsem, bsem, hsem, zsem, usem,
+    pu, zst, lse,
+    big, hid, land, ebuf, pbuf, pw, wg, wu, wd, erl, err, drl, drr,
+    onehot, ids_ref, mst, sst, stats,
+    ring, xsend, xrecv, wsend, wrecv, ssend, srecv, lsem, bsem, hsem,
 ):
     groups, half_rows, dim = hid.shape
     chips = n_tp // CORES
@@ -46,7 +65,13 @@
     hrow = half_rows // 2
     pcols = pw.shape[1] // CORES
     fcols = wg.shape[1] // CORES
-    vocab = zst.shape[1]
+    vocab = zst.shape[2]
+    lanes = stats.shape[3]
+    part = zst.at[:, pl.ds(0, half_rows), pl.ds(0, dim)]
+    width = wg.shape[1]
+    nbuf = onehot.at[pl.ds(0, half_rows), pl.ds(0, dim)]
+    abuf = onehot.at[pl.ds(half_rows, half_rows), pl.ds(0, width)]
+    obuf = onehot.at[:, pl.ds(0, dim)]
     q = big.shape[1]
     n_vq, n_dq = vocab // q, dim // q
 
@@ -198,13 +223,6 @@
         src = lax.rem(me + n_tp - d, n_tp)
         return remote(stats.at[g, src], stats.at[g, src], ssend.at[g, d], srecv.at[g, d], lax.rem(me + d, n_tp))
 
-    def z_copy(g, j):
-        return pltpu.make_async_copy(
-            zst.at[:, pl.ds(j * q, q)], z_h.at[aligned(g, rows), pl.ds(j * q, q)], zsem.at[j])
-
-    def u_copy(g):
-        return pltpu.make_async_copy(pu.at[g], u_h.at[aligned(g, rows)], usem.at[g])
-
     def picks(g):
         @pl.when(g == 0)
         def _():
@@ -212,13 +230,16 @@
                 for j in range(n_dq):
                     emb_copy(i, j).wait()
 
-        ids = tok[aligned(g, rows), :] - me * vocab
-        lanes = ids.shape[1]
-        lane = lax.broadcasted_iota(jnp.int32, ids.shape, 1)
+        per = rows // lanes
+        for i in range(per):
+            row = (tok[pl.ds(g * per + i, 1), :] - me * vocab).astype(F32)
+            ids_ref[i * lanes:(i + 1) * lanes, :] = columns_of(row, lanes)
+        lane = lax.broadcasted_iota(jnp.int32, (rows, lanes), 1).astype(F32)
 
         @pl.loop(0, vocab // lanes)
         def _(j):
-            onehot[:, aligned(j, lanes)] = jnp.where(ids - j * lanes == lane, 1.0, 0.0).astype(BF16)
+            first = (j * lanes).astype(F32)
+            onehot[:, aligned(j, lanes)] = jnp.where(ids_ref[...] == lane + first, 1.0, 0.0).astype(BF16)
 
         tn = tile_of(q, 512)
         for j in range(n_dq):
@@ -246,9 +267,8 @@
     def pick_sum(g):
         pick_swap(g).wait_recv()
 
-        @pl.loop(0, chips)
-        def _(i):
-            r = aligned(i, blk)
+        for i in range(chips):
+            r = pl.ds(i * blk, blk)
             land[g, r, :] = land[g, r, :] + pu[g, pl.ds(pl.multiple_of(k * half_rows + i * blk, blk), blk), :]
 
         rs_first(E_RS, land, e_lands, g)
@@ -261,10 +281,10 @@
     def h_norm(g):
         hid_copy(g).wait()
 
-        @pl.loop(0, chips)
-        def _(i):
-            r = aligned(i, blk)
-            hid[g, r, :] = norm_rows(hid[g, r, :], hg[...]).astype(BF16)
+        def put(r, v):
+            hid[g, r, :] = v
+
+        norm_into(lambda r: hid[g, r, :], put, hg, half_rows)
 
         @pl.when(g == 0)
         def _():
@@ -285,30 +305,33 @@
         pbuf[g, :, aligned(z, CORES * pcols)] = out.astype(BF16)
         ag_send(P_AG, p_blk, g, 1)
 
-    def feed_forward(g):
-        for cp in ag_wait(P_AG, p_blk, g, hops):
-            cp.wait_recv()
-
-        @pl.when(g == 0)
-        def _():
-            for i in range(1, 4):
-                w_recv[i].wait_recv()
-
-        @pl.loop(0, chips)
-        def _(i):
-            r = aligned(i, blk)
-            nbuf[r, :] = norm_rows(pbuf[g, r, :], fg[...]).astype(BF16)
-
-        width = wg.shape[1]
+    def ffn_up(g, first):
+        if first:
+            for cp in ag_wait(P_AG, p_blk, g, hops):
+                cp.wait_recv()
+
+            @pl.when(g == 0)
+            def _():
+                for i in range(1, 4):
+                    w_recv[i].wait_recv()
+
+            def put(r, v):
+                nbuf[r, :] = v
+
+            norm_into(lambda r: pbuf[g, r, :], put, fg, half_rows)
+
         tn = tile_of(width, 256)
-
-        @pl.loop(0, width // tn)
+        n = width // tn
+        lo, hi = (0, n // 2) if first else (n // 2, n)
+
+        @pl.loop(lo, hi)
         def _(t):
             c = aligned(t, tn)
             gate = jnp.dot(nbuf[...], wg[:, c], preferred_element_type=F32)
             up = jnp.dot(nbuf[...], wu[:, c], preferred_element_type=F32)
             abuf[:, c] = (jax.nn.silu(gate) * up).astype(BF16)
 
+    def ffn_down(g):
         tm = tile_of(dim, 512)
 
         @pl.loop(0, dim // tm)
@@ -319,6 +342,8 @@
         rs_first(D_RS, part, d_lands, g)
 
     def new_u(g):
+        for cp in rs_pair(D_RS, part, d_lands, g, 1):
+            cp.wait_send()
         total = rs_sum(D_RS, part, d_lands, g)
         total = pbuf[g, aligned(z, blk), :].astype(F32) + total
         pu[g, pl.ds(pl.multiple_of(k * half_rows + z * blk, blk), blk), :] = total.astype(BF16)
@@ -329,48 +354,44 @@
             cp.wait_recv()
         u_swap(g, k).start()
 
-    def head(g):
-        u_swap(g, other).wait_recv()
-        u_copy(g).start()
-
-        @pl.when(g == 0)
-        def _():
+    def head(g, j):
+        if j == 0:
+            u_swap(g, other).wait_recv()
+
+            @pl.when(g == 0)
+            def _():
+                for i in range(n_dq):
+                    for jj in range(n_vq):
+                        head_copy(i, jj).wait()
+
+            def put(r, v):
+                obuf[r, :] = v
+
+            norm_into(lambda r: pu[g, r, :], put, og, rows)
+
+        tn = tile_of(q, 512)
+
+        @pl.loop(0, q // tn)
+        def _(t):
+            acc = None
             for i in range(n_dq):
-                for j in range(n_vq):
-                    head_copy(i, j).wait()
-
-        @pl.loop(0, rows // blk)
+                d = jnp.dot(obuf[:, i * q:(i + 1) * q], big[i * n_vq + j, :, aligned(t, tn)], preferred_element_type=F32)
+                acc = d if acc is None else acc + d
+            zst[g, :, pl.ds(pl.multiple_of(j * q + t * tn, tn), tn)] = acc
+
+    def row_stats(g):
+        unit, wide = 8, 8
+
+        @pl.loop(0, rows // (unit * wide))
         def _(i):
-            r = aligned(i, blk)
-            obuf[r, :] = norm_rows(pu[g, r, :], og[...]).astype(BF16)
-
-        tn = tile_of(q, 512)
-        for j in range(n_vq):
-            @pl.when(g > 0)
-            def _():
-                z_copy(g - 1, j).wait()
-
-            @pl.loop(0, q // tn)
-            def _(t):
-                acc = None
-                for i in range(n_dq):
-                    d = jnp.dot(obuf[:, i * q:(i + 1) * q], big[i * n_vq + j, :, aligned(t, tn)], preferred_element_type=F32)
-                    acc = d if acc is None else acc + d
-                zst[:, pl.ds(pl.multiple_of(j * q + t * tn, tn), tn)] = acc
-
-            z_copy(g, j).start()
-
-        @pl.loop(0, rows // blk)
-        def _(i):
-            r = aligned(i, blk)
-            zz = zst[r, :]
-            m = jnp.max(zz, axis=-1, keepdims=True)
-            s = jnp.sum(jnp.exp(zz - m), axis=-1, keepdims=True)
-            mst[r, :] = jnp.broadcast_to(m, (blk, mst.shape[1]))
-            sst[r, :] = jnp.broadcast_to(s, (blk, sst.shape[1]))
+            rr = [pl.ds(pl.multiple_of((i * wide + u) * unit, unit), unit) for u in range(wide)]
+            tops = [jnp.max(zst[g, r, :], axis=-1, keepdims=True) for r in rr]
+            for r, m in zip(rr, tops):
+                s = jnp.sum(jnp.exp(zst[g, r, :] - m), axis=-1, keepdims=True)
+                mst[r, :] = jnp.broadcast_to(m, (unit, lanes))
+                sst[r, :] = jnp.broadcast_to(s, (unit, lanes))
 
         mt, st = mst[...].T, sst[...].T
-        lanes = stats.shape[3]
         n = rows // lanes
         for i in range(n):
             c = slice(i * lanes, (i + 1) * lanes)
@@ -382,56 +403,96 @@
     def total_lse(g):
         for d in range(1, n_tp):
             stat_wait(g, d).wait_recv()
-        n = rows // stats.shape[3]
+        n = rows // lanes
         ms = [stats[g, i, 0:n, :] for i in range(n_tp)]
         top = functools.reduce(jnp.maximum, ms)
         tot = functools.reduce(jnp.add, [stats[g, i, n:2 * n, :] * jnp.exp(ms[i] - top) for i in range(n_tp)])
-        lse[g, 0:n, :] = top + jnp.log(tot)
-
-    stages = [picks, pick_sum]
-    stages += [functools.partial(rs_step, E_RS, land, e_lands, s=s) for s in range(2, hops + 1)]
-    stages += [e_norm]
-    stages += [functools.partial(ag_step, E_AG, e_blk, s=s) for s in range(2, hops + 1)]
-    h_at = len(stages) - 1
-    stages += [project]
-    stages += [functools.partial(ag_step, P_AG, p_blk, s=s) for s in range(2, hops + 1)]
-    stages += [feed_forward]
-    stages += [functools.partial(rs_step, D_RS, part, d_lands, s=s) for s in range(2, hops + 1)]
-    stages += [new_u]
-    stages += [functools.partial(ag_step, U_AG, u_blk, s=s) for s in range(2, hops + 1)]
-    stages += [u_done]
-    head_at = len(stages)
-    stages += [head, total_lse]
-    order = [i for i in range(len(stages) - 1, -1, -1) if i not in (head_at,)] + [head_at]
+        total = top + jnp.log(tot)
+        for i in range(n):
+            lse[g, i * lanes:(i + 1) * lanes, :] = columns_of(total[i:i + 1, :], lanes)
+
+    bind = functools.partial
+    stages = [[picks], [pick_sum]]
+    stages += [[bind(rs_step, E_RS, land, e_lands, s=s)] for s in range(2, hops + 1)]
+    stages += [[e_norm]]
+    stages += [[bind(ag_step, E_AG, e_blk, s=s)] for s in range(2, hops + 1)]
+    stages[-1].append(h_norm)
+    stages += [[project]]
+    stages += [[bind(ag_step, P_AG, p_blk, s=s)] for s in range(2, hops + 1)]
+    stages += [[bind(ffn_up, first=True), bind(ffn_up, first=False), ffn_down]]
+    stages += [[bind(rs_step, D_RS, part, d_lands, s=s)] for s in range(2, hops + 1)]
+    stages += [[new_u]]
+    stages += [[bind(ag_step, U_AG, u_blk, s=s)] for s in range(2, hops + 1)]
+    stages += [[u_done]]
+    stages += [[bind(head, j=j) for j in range(n_vq)] + [row_stats]]
+    stages += [[total_lse]]
+    order = sorted((-i + p, p > 0, i, p) for i, pieces in enumerate(stages) for p in range(len(pieces)))
 
     @pl.loop(0, groups + len(stages) - 1)
     def _(t):
-        for i in order:
+        for _, _, i, p in order:
             g = t - i
 
             @pl.when((g >= 0) & (g < groups))
             def _():
-                stages[i](g=g)
-                if i == h_at:
-                    h_norm(g)
+                stages[i][p](g=g)
 
     for cp in w_send:
         cp.wait_send()
-    for j in range(n_vq):
-        z_copy(groups - 1, j).wait()
 
     @pl.loop(0, groups)
     def _(g):
         for s in range(1, hops + 1):
-            for cp in rs_pair(E_RS, land, e_lands, g, s) + rs_pair(D_RS, part, d_lands, g, s):
+            for cp in rs_pair(E_RS, land, e_lands, g, s):
                 cp.wait_send()
+            if s > 1:
+                for cp in rs_pair(D_RS, part, d_lands, g, s):
+                    cp.wait_send()
             for c, b in ((E_AG, e_blk), (P_AG, p_blk), (U_AG, u_blk)):
                 for cp in ag_pair(c, b, g, s):
                     cp.wait_send()
         u_swap(g, k).wait_send()
         for d in range(1, n_tp):
             stat_send(g, d).wait_send()
-        u_copy(g).wait()
+
+
+def finish_kernel(z, lse, pu, logp, u, sem):
+    i = pl.program_id(0)
+    n_rows, vocab = logp.shape
+    unit, lanes = 16, lse.shape[1]
+    u_copy = pltpu.make_async_copy(pu, u, sem)
+
+    @pl.when(i == 0)
+    def _():
+        u_copy.start()
+
+    @pl.loop(0, n_rows // unit)
+    def _(c):
+        r = aligned(i * (n_rows // unit) + c, unit)
+        base = lse[r, :]
+        for j in range(vocab // lanes):
+            cols = slice(j * lanes, (j + 1) * lanes)
+            logp[aligned(c, unit), cols] = z[r, cols] - base
+
+    @pl.when(i == pl.num_programs(0) - 1)
+    def _():
+        u_copy.wait()
+
+
+def finish_call(z, lse, pu):
+    batch, vocab = z.shape
+    vm = pl.BlockSpec(memory_space=pltpu.VMEM)
+    step = GROUP_ROWS // CORES
+    return pl.pallas_call(
+        finish_kernel,
+        grid=(batch // step,),
+        out_shape=(jax.ShapeDtypeStruct((batch, vocab), F32), jax.ShapeDtypeStruct(pu.shape, BF16)),
+        in_specs=[vm, vm, vm],
+        out_specs=(pl.BlockSpec((step, vocab), lambda i: (i, 0)), pl.BlockSpec(memory_space=pltpu.HBM)),
+        scratch_shapes=[pltpu.SemaphoreType.DMA],
+        compiler_params=pltpu.CompilerParams(vmem_limit_bytes=6 << 20),
+        name="finish",
+    )(z, lse, pu)
 
 
 def draft_call(n_tp, hidden, tokens, embedding, head_w, h_norm, e_norm, f_norm, o_norm, proj_w, w_gate, w_up, w_down):
@@ -445,29 +506,27 @@
     blk = half_rows // chips
     q = dim // 2
     lanes = 128
-    tok = jnp.broadcast_to(tokens[:, None], (batch, lanes))
+    tok = tokens.reshape(batch // lanes, lanes)
     vm = pl.BlockSpec(memory_space=pltpu.VMEM)
-    anyspec = pl.BlockSpec(memory_space=pl.ANY)
+    hbm = pl.BlockSpec(memory_space=pltpu.HBM)
     dma = pltpu.SemaphoreType.DMA
     n_big = (vocab // q) * (dim // q)
     flops = 2 * batch * (2 * dim * vocab + 2 * dim * pcols + 3 * dim * fcols)
     return pl.pallas_call(
         functools.partial(step_kernel, n_tp),
         out_shape=(
-            jax.ShapeDtypeStruct((batch, dim), BF16),
-            jax.ShapeDtypeStruct((batch, vocab), F32),
-            jax.ShapeDtypeStruct((groups, 8, lanes), F32),
+            pltpu.VMEM((groups, GROUP_ROWS, dim), BF16),
+            pltpu.VMEM((groups, GROUP_ROWS, vocab), F32),
+            pltpu.VMEM((groups, GROUP_ROWS, lanes), F32),
         ),
-        in_specs=[vm] * 5 + [anyspec] * 7,
-        out_specs=(anyspec, anyspec, vm),
+        in_specs=[vm] * 5 + [hbm] * 7,
+        out_specs=(vm, vm, vm),
         scratch_shapes=[
             pltpu.VMEM((n_big, q, q), BF16),
             pltpu.VMEM((groups, half_rows, dim), BF16),
-            pltpu.VMEM((groups, GROUP_ROWS, dim), BF16),
             pltpu.VMEM((groups, half_rows, dim), BF16),
             pltpu.VMEM((groups, half_rows, dim), BF16),
             pltpu.VMEM((groups, half_rows, dim), BF16),
-            pltpu.VMEM((groups, half_rows, dim), F32),
             pltpu.VMEM((2 * dim, CORES * pcols), BF16),
             pltpu.VMEM((dim, CORES * fcols), BF16),
             pltpu.VMEM((dim, CORES * fcols), BF16),
@@ -477,10 +536,7 @@
             pltpu.VMEM((groups, hops, blk, dim), F32),
             pltpu.VMEM((groups, hops, blk, dim), F32),
             pltpu.VMEM((GROUP_ROWS, vocab), BF16),
-            pltpu.VMEM((half_rows, dim), BF16),
-            pltpu.VMEM((half_rows, CORES * fcols), BF16),
-            pltpu.VMEM((GROUP_ROWS, dim), BF16),
-            pltpu.VMEM((GROUP_ROWS, vocab), F32),
+            pltpu.VMEM((GROUP_ROWS, lanes), F32),
             pltpu.VMEM((GROUP_ROWS, lanes), F32),
             pltpu.VMEM((GROUP_ROWS, lanes), F32),
             pltpu.VMEM((groups, n_tp, 8, lanes), F32),
@@ -494,11 +550,9 @@
             dma((4 + groups,)),
             dma((n_big,)),
             dma((n_big,)),
-            dma((vocab // q,)),
-            dma((groups,)),
         ],
         compiler_params=pltpu.CompilerParams(
-            collective_id=0, has_side_effects=True, vmem_limit_bytes=67043328),
+            collective_id=0, has_side_effects=True, vmem_limit_bytes=KERNEL_VMEM),
         cost_estimate=pl.CostEstimate(flops=flops, bytes_accessed=70 << 20, transcendentals=0),
         name="draft_step",
     )(tok, h_norm[None], e_norm[None], f_norm[None], o_norm[None], hidden, embedding, head_w, proj_w, w_gate, w_up, w_down)
@@ -508,10 +562,10 @@
     n_tp = mesh.shape["tp"]
 
     def draft_step(hidden, *rest):
-        new_u, logits, lse = draft_call(n_tp, hidden, *rest)
-        groups = lse.shape[0]
-        lse_rows = lse[:, : GROUP_ROWS // lse.shape[2], :].reshape(hidden.shape[0])
-        return new_u, logits - lse_rows[:, None]
+        batch, dim = hidden.shape
+        pu, z, lse = draft_call(n_tp, hidden, *rest)
+        logp, new_u = finish_call(z.reshape(batch, -1), lse.reshape(batch, -1), pu.reshape(batch, dim))
+        return new_u, logp
 
     specs_in = (P("dp", None), P("dp"), P("tp", None), P(None, "tp"), P(None), P(None), P(None), P(None), P(None, "tp"), P(None, "tp"), P(None, "tp"), P("tp", None))
     specs_out = (P("dp", None), P("dp", "tp"))

time: 235 us -> 205 us (0.87)
  Pallas kernels: 217 us -> 204 us
  other arithmetic: 12 us -> 0 us
  local copies, waits for them, and re-layouts: 4.42 us -> 0 us
    pallas_call x1 -> x2, Pallas kernels: 217 us -> 204 us  [the longest x1 198 us: draft_call(): pl.pallas_call(functools.partial(step_kernel, n_tp), out_shape=(pltpu.VME...]
    sub x1 -> x0, other arithmetic: 12 us -> none  [draft_step(): return (new_u, logits - lse_rows[:, None])]
where the time goes in v2:
time: 205 us
  Pallas kernels  204 us (100%)
    pallas_call x1, Pallas kernels, draft_call(): pl.pallas_call(functools.partial(step_kernel, n_tp), out_shape=(pltpu.VME...  198 us
    pallas_call x1, Pallas kernels, finish_call(): pl.pallas_call(finish_kernel, grid=(batch // step,), out_shape=(jax.Shape...  6.87 us

profile of v2, /device:TPU:21, one launch (start us, length us, event | category | flops | bytes accessed | tf_op | source)
XLA Modules:
  0.0 205.1 jit_solution(4460920054149317611)
XLA Ops:
  0.6 197.6 %draft_step.1 = (bf16[4,256,2048]{2,1,0:T(8,128)(2,1)S(1)}, f32[4,256,3072]{2,1,0:T(8,128)S(1)}, f32[4,256,128]{2,1,0:T(8,128)S(1)}) custom-call(s32[8,128]{1,0:T(8,128)} %bitcast.15, f32[1,2048]{1,0:T(1,128)} %bitcast.11, f32[1,2048]{1,0:T(1,128)} %bitcast.12, f32[1,2048]{1,0:T(1,128)} %bitcast.13, f32[1,2048]{1,0:T(1,128)} %bitcast.14, ...), custom_call_target="tpu_custom_call" | custom-call | flops 33285996544 | bytes 73400320 | tf_op jit(solution)/shard_map/draft_step/pallas_call | solution.py:515
  198.2 6.9 %finish.1 = (f32[1024,3072]{1,0:T(8,128)}, bf16[1024,2048]{1,0:T(8,128)(2,1)}) custom-call(f32[1024,3072]{1,0:T(8,128)S(1)} %bitcast.8, f32[1024,128]{1,0:T(8,128)S(1)} %bitcast.10, bf16[1024,2048]{1,0:T(8,128)(2,1)S(1)} %bitcast.9), custom_call_target="tpu_custom_call" | custom-call | tf_op jit(solution)/shard_map/finish/pallas_call | solution.py:486

commit v3 on v2

--- a/solution.py
+++ b/solution.py
@@ -11,6 +11,7 @@
 BF16 = jnp.bfloat16
 F32 = jnp.float32
 GROUP_ROWS = 256
+LOWEST = -3e38
 KERNEL_VMEM = 46 << 20
 CORES = 2
 SEND_R, SEND_L, FROM_L, FROM_R = range(4)
@@ -116,20 +117,12 @@
     w_send = [remote(r, r, wsend.at[i], wrecv.at[i], sib) for i, r in enumerate([own_pw, own_wg, own_wu, own_wd])]
     w_recv = [remote(r, r, wsend.at[i], wrecv.at[i], sib) for i, r in enumerate([oth_pw, oth_wg, oth_wu, oth_wd])]
 
-    for i in range(n_vq):
-        for j in range(n_dq):
-            emb_copy(i, j).start()
-    for c in w_local:
-        c.start()
-
-    @pl.loop(0, groups)
-    def _(g):
-        hid_copy(g).start()
-
     barrier = pltpu.get_barrier_semaphore()
     for d in range(1, n_tp):
         pl.semaphore_signal(barrier, inc=1, device_id={"tp": lax.rem(me + d, n_tp)}, device_id_type=pl.DeviceIdType.MESH)
-    pl.semaphore_wait(barrier, n_tp - 1)
+    for j in range(n_dq):
+        for i in range(n_vq):
+            emb_copy(i, j).start()
 
     def e_blk(g, o, h):
         cols = pl.ds(0, dim) if h is None else pl.ds(h * hcol, hcol)
@@ -223,46 +216,44 @@
         src = lax.rem(me + n_tp - d, n_tp)
         return remote(stats.at[g, src], stats.at[g, src], ssend.at[g, d], srecv.at[g, d], lax.rem(me + d, n_tp))
 
-    def picks(g):
-        @pl.when(g == 0)
-        def _():
-            for i in range(n_vq):
-                for j in range(n_dq):
-                    emb_copy(i, j).wait()
-
+    def one_hot(g):
         per = rows // lanes
         for i in range(per):
             row = (tok[pl.ds(g * per + i, 1), :] - me * vocab).astype(F32)
             ids_ref[i * lanes:(i + 1) * lanes, :] = columns_of(row, lanes)
-        lane = lax.broadcasted_iota(jnp.int32, (rows, lanes), 1).astype(F32)
-
-        @pl.loop(0, vocab // lanes)
+        lane = lax.broadcasted_iota(jnp.int32, (rows, lanes), 1)
+
+        @pl.loop(0, vocab // lanes, unroll=4)
         def _(j):
-            first = (j * lanes).astype(F32)
-            onehot[:, aligned(j, lanes)] = jnp.where(ids_ref[...] == lane + first, 1.0, 0.0).astype(BF16)
-
+            here = (lane + j * lanes).astype(F32)
+            onehot[:, aligned(j, lanes)] = jnp.where(ids_ref[...] == here, 1.0, 0.0).astype(BF16)
+
+    def pick_cols(g, j):
         tn = tile_of(q, 512)
-        for j in range(n_dq):
-            @pl.loop(0, q // tn)
-            def _(t):
-                acc = None
-                for i in range(n_vq):
-                    d = jnp.dot(onehot[:, i * q:(i + 1) * q], big[i * n_dq + j, :, aligned(t, tn)], preferred_element_type=F32)
-                    acc = d if acc is None else acc + d
-                pu[g, :, pl.ds(pl.multiple_of(j * q + t * tn, tn), tn)] = acc.astype(BF16)
-
-        pick_swap(g).start()
-
-        @pl.when(g == groups - 1)
+
+        @pl.loop(0, q // tn)
+        def _(t):
+            acc = None
+            for i in range(n_vq):
+                d = jnp.dot(onehot[:, i * q:(i + 1) * q], big[i * n_dq + j, :, aligned(t, tn)], preferred_element_type=F32)
+                acc = d if acc is None else acc + d
+            pu[g, :, pl.ds(pl.multiple_of(j * q + t * tn, tn), tn)] = acc.astype(BF16)
+
+    def picks(g, j):
+        @pl.when(g > 0)
         def _():
-            for i in range(n_dq):
-                for j in range(n_vq):
-                    head_copy(i, j).start()
-
-        @pl.when(g == 0)
-        def _():
-            w_local[0].wait()
-            w_send[0].start()
+            if j == 0:
+                one_hot(g)
+            pick_cols(g, j)
+            if j == n_dq - 1:
+                pick_swap(g).start()
+
+        if j == n_dq - 1:
+            @pl.when(g == groups - 1)
+            def _():
+                for i in range(n_dq):
+                    for jj in range(n_vq):
+                        head_copy(i, jj).start()
 
     def pick_sum(g):
         pick_swap(g).wait_recv()
@@ -354,7 +345,23 @@
             cp.wait_recv()
         u_swap(g, k).start()
 
+    def lane_stats(g, first, n):
+        unit = 16
+
+        @pl.loop(0, rows // unit, unroll=2)
+        def _(i):
+            r = aligned(i, unit)
+            parts = [zst[g, r, pl.ds(pl.multiple_of(first + b * lanes, lanes), lanes)] for b in range(n // lanes)]
+            old = mst[r, :]
+            top = functools.reduce(jnp.maximum, parts, old)
+            total = sst[r, :] * jnp.exp(old - top)
+            for v in parts:
+                total += jnp.exp(v - top)
+            mst[r, :] = top
+            sst[r, :] = total
+
     def head(g, j):
+        tn = tile_of(q, 512)
         if j == 0:
             u_swap(g, other).wait_recv()
 
@@ -368,8 +375,8 @@
                 obuf[r, :] = v
 
             norm_into(lambda r: pu[g, r, :], put, og, rows)
-
-        tn = tile_of(q, 512)
+            mst[...] = jnp.full(mst.shape, LOWEST, F32)
+            sst[...] = jnp.zeros(sst.shape, F32)
 
         @pl.loop(0, q // tn)
         def _(t):
@@ -378,20 +385,14 @@
                 d = jnp.dot(obuf[:, i * q:(i + 1) * q], big[i * n_vq + j, :, aligned(t, tn)], preferred_element_type=F32)
                 acc = d if acc is None else acc + d
             zst[g, :, pl.ds(pl.multiple_of(j * q + t * tn, tn), tn)] = acc
+            lane_stats(g, j * q + t * tn, tn)
 
     def row_stats(g):
-        unit, wide = 8, 8
-
-        @pl.loop(0, rows // (unit * wide))
-        def _(i):
-            rr = [pl.ds(pl.multiple_of((i * wide + u) * unit, unit), unit) for u in range(wide)]
-            tops = [jnp.max(zst[g, r, :], axis=-1, keepdims=True) for r in rr]
-            for r, m in zip(rr, tops):
-                s = jnp.sum(jnp.exp(zst[g, r, :] - m), axis=-1, keepdims=True)
-                mst[r, :] = jnp.broadcast_to(m, (unit, lanes))
-                sst[r, :] = jnp.broadcast_to(s, (unit, lanes))
-
-        mt, st = mst[...].T, sst[...].T
+        m = mst[...]
+        top = jnp.max(m, axis=-1, keepdims=True)
+        s = jnp.sum(sst[...] * jnp.exp(m - top), axis=-1, keepdims=True)
+        mt = jnp.broadcast_to(top, mst.shape).T
+        st = jnp.broadcast_to(s, sst.shape).T
         n = rows // lanes
         for i in range(n):
             c = slice(i * lanes, (i + 1) * lanes)
@@ -412,7 +413,7 @@
             lse[g, i * lanes:(i + 1) * lanes, :] = columns_of(total[i:i + 1, :], lanes)
 
     bind = functools.partial
-    stages = [[picks], [pick_sum]]
+    stages = [[bind(picks, j=j) for j in range(n_dq)], [pick_sum]]
     stages += [[bind(rs_step, E_RS, land, e_lands, s=s)] for s in range(2, hops + 1)]
     stages += [[e_norm]]
     stages += [[bind(ag_step, E_AG, e_blk, s=s)] for s in range(2, hops + 1)]
@@ -426,11 +427,35 @@
     stages += [[u_done]]
     stages += [[bind(head, j=j) for j in range(n_vq)] + [row_stats]]
     stages += [[total_lse]]
-    order = sorted((-i + p, p > 0, i, p) for i, pieces in enumerate(stages) for p in range(len(pieces)))
-
-    @pl.loop(0, groups + len(stages) - 1)
+    last = len(stages) - 1
+    order = []
+    for i, pieces in enumerate(stages):
+        for p in range(len(pieces)):
+            place = (1.0 if i == last else -1.5 if (i, p) == (0, 0) else -i + p * 1.0, p > 0)
+            order.append((place, i, p))
+    order.sort()
+
+    one_hot(0)
+    for j in range(n_dq):
+        for i in range(n_vq):
+            emb_copy(i, j).wait()
+        if j == n_dq - 1:
+            for c in w_local:
+                c.start()
+
+            @pl.loop(0, groups)
+            def _(g):
+                hid_copy(g).start()
+
+        pick_cols(0, j)
+    pl.semaphore_wait(barrier, n_tp - 1)
+    pick_swap(0).start()
+    w_local[0].wait()
+    w_send[0].start()
+
+    @pl.loop(1, groups + last)
     def _(t):
-        for _, _, i, p in order:
+        for _, i, p in order:
             g = t - i
 
             @pl.when((g >= 0) & (g < groups))
@@ -482,7 +507,7 @@
 def finish_call(z, lse, pu):
     batch, vocab = z.shape
     vm = pl.BlockSpec(memory_space=pltpu.VMEM)
-    step = GROUP_ROWS // CORES
+    step = GROUP_ROWS
     return pl.pallas_call(
         finish_kernel,
         grid=(batch // step,),
@@ -490,7 +515,7 @@
         in_specs=[vm, vm, vm],
         out_specs=(pl.BlockSpec((step, vocab), lambda i: (i, 0)), pl.BlockSpec(memory_space=pltpu.HBM)),
         scratch_shapes=[pltpu.SemaphoreType.DMA],
-        compiler_params=pltpu.CompilerParams(vmem_limit_bytes=6 << 20),
+        compiler_params=pltpu.CompilerParams(vmem_limit_bytes=16 << 20),
         name="finish",
     )(z, lse, pu)
 

time: 205 us -> 186 us (0.907)
  Pallas kernels: 204 us -> 185 us
    pallas_call x1, Pallas kernels: 198 us -> 179 us  [draft_call(): pl.pallas_call(functools.partial(step_kernel, n_tp), out_shape=(pltpu.VME...]
where the time goes in v3:
time: 186 us; the launch traced here: 185 us
  Pallas kernels  185 us (99%)
    pallas_call x1, Pallas kernels, draft_call(): pl.pallas_call(functools.partial(step_kernel, n_tp), out_shape=(pltpu.VME...  179 us
    pallas_call x1, Pallas kernels, finish_call(): pl.pallas_call(finish_kernel, grid=(batch // step,), out_shape=(jax.Shape...  5.97 us

profile of v3, /device:TPU:21, one launch (start us, length us, event | category | flops | bytes accessed | tf_op | source)
XLA Modules:
  0.0 185.4 jit_solution(13317249579339213818)
XLA Ops:
  0.6 178.8 %draft_step.1 = (bf16[4,256,2048]{2,1,0:T(8,128)(2,1)S(1)}, f32[4,256,3072]{2,1,0:T(8,128)S(1)}, f32[4,256,128]{2,1,0:T(8,128)S(1)}) custom-call(s32[8,128]{1,0:T(8,128)} %bitcast.15, f32[1,2048]{1,0:T(1,128)} %bitcast.11, f32[1,2048]{1,0:T(1,128)} %bitcast.12, f32[1,2048]{1,0:T(1,128)} %bitcast.13, f32[1,2048]{1,0:T(1,128)} %bitcast.14, ...), custom_call_target="tpu_custom_call" | custom-call | flops 33285996544 | bytes 73400320 | tf_op jit(solution)/shard_map/draft_step/pallas_call | solution.py:540
  179.4 6.0 %finish.1 = (f32[1024,3072]{1,0:T(8,128)}, bf16[1024,2048]{1,0:T(8,128)(2,1)}) custom-call(f32[1024,3072]{1,0:T(8,128)S(1)} %bitcast.8, f32[1024,128]{1,0:T(8,128)S(1)} %bitcast.10, bf16[1024,2048]{1,0:T(8,128)(2,1)S(1)} %bitcast.9), custom_call_target="tpu_custom_call" | custom-call | tf_op jit(solution)/shard_map/finish/pallas_call | solution.py:511

commit v4 on v3

--- a/solution.py
+++ b/solution.py
@@ -11,7 +11,6 @@
 BF16 = jnp.bfloat16
 F32 = jnp.float32
 GROUP_ROWS = 256
-LOWEST = -3e38
 KERNEL_VMEM = 46 << 20
 CORES = 2
 SEND_R, SEND_L, FROM_L, FROM_R = range(4)
@@ -94,11 +93,11 @@
 
     def emb_copy(i, j):
         return pltpu.make_async_copy(
-            emb_h.at[pl.ds(i * q, q), pl.ds(j * q, q)], big.at[i * n_dq + j], bsem.at[i * n_dq + j])
+            emb_h.at[pl.ds(i * q, q), pl.ds(j * q, q)], big.at[j * n_vq + i], bsem.at[j * n_vq + i])
 
     def head_copy(i, j):
         return pltpu.make_async_copy(
-            head_h.at[pl.ds(i * q, q), pl.ds(j * q, q)], big.at[i * n_vq + j], hsem.at[i * n_vq + j])
+            head_h.at[pl.ds(i * q, q), pl.ds(j * q, q)], big.at[j * n_dq + i], hsem.at[j * n_dq + i])
 
     def hid_copy(g):
         return pltpu.make_async_copy(
@@ -229,14 +228,12 @@
             onehot[:, aligned(j, lanes)] = jnp.where(ids_ref[...] == here, 1.0, 0.0).astype(BF16)
 
     def pick_cols(g, j):
-        tn = tile_of(q, 512)
+        tn = tile_of(q, 1024)
 
         @pl.loop(0, q // tn)
         def _(t):
-            acc = None
-            for i in range(n_vq):
-                d = jnp.dot(onehot[:, i * q:(i + 1) * q], big[i * n_dq + j, :, aligned(t, tn)], preferred_element_type=F32)
-                acc = d if acc is None else acc + d
+            table = big[j * n_vq:(j + 1) * n_vq, :, aligned(t, tn)].reshape(vocab, tn)
+            acc = jnp.dot(onehot[...], table, preferred_element_type=F32)
             pu[g, :, pl.ds(pl.multiple_of(j * q + t * tn, tn), tn)] = acc.astype(BF16)
 
     def picks(g, j):
@@ -345,23 +342,27 @@
             cp.wait_recv()
         u_swap(g, k).start()
 
-    def lane_stats(g, first, n):
+    head_tn = tile_of(q, 512)
+    per_piece = q // head_tn
+
+    def lane_stats(g, tile):
         unit = 16
-
-        @pl.loop(0, rows // unit, unroll=2)
-        def _(i):
-            r = aligned(i, unit)
-            parts = [zst[g, r, pl.ds(pl.multiple_of(first + b * lanes, lanes), lanes)] for b in range(n // lanes)]
-            old = mst[r, :]
-            top = functools.reduce(jnp.maximum, parts, old)
-            total = sst[r, :] * jnp.exp(old - top)
+        for i in range(rows // unit):
+            r = slice(i * unit, (i + 1) * unit)
+            parts = [zst[g, r, tile * head_tn + b * lanes:tile * head_tn + (b + 1) * lanes] for b in range(head_tn // lanes)]
+            top = functools.reduce(jnp.maximum, parts)
+            if tile == 0:
+                total = jnp.zeros_like(top)
+            else:
+                old = mst[r, :]
+                top = jnp.maximum(top, old)
+                total = sst[r, :] * jnp.exp(old - top)
             for v in parts:
                 total += jnp.exp(v - top)
             mst[r, :] = top
             sst[r, :] = total
 
     def head(g, j):
-        tn = tile_of(q, 512)
         if j == 0:
             u_swap(g, other).wait_recv()
 
@@ -375,19 +376,17 @@
                 obuf[r, :] = v
 
             norm_into(lambda r: pu[g, r, :], put, og, rows)
-            mst[...] = jnp.full(mst.shape, LOWEST, F32)
-            sst[...] = jnp.zeros(sst.shape, F32)
-
-        @pl.loop(0, q // tn)
-        def _(t):
-            acc = None
-            for i in range(n_dq):
-                d = jnp.dot(obuf[:, i * q:(i + 1) * q], big[i * n_vq + j, :, aligned(t, tn)], preferred_element_type=F32)
-                acc = d if acc is None else acc + d
-            zst[g, :, pl.ds(pl.multiple_of(j * q + t * tn, tn), tn)] = acc
-            lane_stats(g, j * q + t * tn, tn)
+
+        for t in range(per_piece):
+            tile = j * per_piece + t
+            if tile > 0:
+                lane_stats(g, tile - 1)
+            weights = big[j * n_dq:(j + 1) * n_dq, :, t * head_tn:(t + 1) * head_tn].reshape(dim, head_tn)
+            acc = jnp.dot(obuf[...], weights, preferred_element_type=F32)
+            zst[g, :, tile * head_tn:(tile + 1) * head_tn] = acc
 
     def row_stats(g):
+        lane_stats(g, n_vq * per_piece - 1)
         m = mst[...]
         top = jnp.max(m, axis=-1, keepdims=True)
         s = jnp.sum(sst[...] * jnp.exp(m - top), axis=-1, keepdims=True)

time: 186 us -> 177 us (0.952)
  Pallas kernels: 185 us -> 176 us
    pallas_call x1, Pallas kernels: 179 us -> 170 us  [draft_call(): pl.pallas_call(functools.partial(step_kernel, n_tp), out_shape=(pltpu.VME...]
where the time goes in v4:
time: 177 us
  Pallas kernels  176 us (99%)
    pallas_call x1, Pallas kernels, draft_call(): pl.pallas_call(functools.partial(step_kernel, n_tp), out_shape=(pltpu.VME...  170 us
    pallas_call x1, Pallas kernels, finish_call(): pl.pallas_call(finish_kernel, grid=(batch // step,), out_shape=(jax.Shape...  5.97 us

profile of v4, /device:TPU:21, one launch (start us, length us, event | category | flops | bytes accessed | tf_op | source)
XLA Modules:
  0.0 176.8 jit_solution(2448537494655916441)
XLA Ops:
  0.6 170.1 %draft_step.1 = (bf16[4,256,2048]{2,1,0:T(8,128)(2,1)S(1)}, f32[4,256,3072]{2,1,0:T(8,128)S(1)}, f32[4,256,128]{2,1,0:T(8,128)S(1)}) custom-call(s32[8,128]{1,0:T(8,128)} %bitcast.15, f32[1,2048]{1,0:T(1,128)} %bitcast.11, f32[1,2048]{1,0:T(1,128)} %bitcast.12, f32[1,2048]{1,0:T(1,128)} %bitcast.13, f32[1,2048]{1,0:T(1,128)} %bitcast.14, ...), custom_call_target="tpu_custom_call" | custom-call | flops 33285996544 | bytes 73400320 | tf_op jit(solution)/shard_map/draft_step/pallas_call | solution.py:539
  170.8 6.0 %finish.1 = (f32[1024,3072]{1,0:T(8,128)}, bf16[1024,2048]{1,0:T(8,128)(2,1)}) custom-call(f32[1024,3072]{1,0:T(8,128)S(1)} %bitcast.8, f32[1024,128]{1,0:T(8,128)S(1)} %bitcast.10, bf16[1024,2048]{1,0:T(8,128)(2,1)S(1)} %bitcast.9), custom_call_target="tpu_custom_call" | custom-call | tf_op jit(solution)/shard_map/finish/pallas_call | solution.py:510

commit v5 on v4

--- a/solution.py
+++ b/solution.py
@@ -11,7 +11,7 @@
 BF16 = jnp.bfloat16
 F32 = jnp.float32
 GROUP_ROWS = 256
-KERNEL_VMEM = 46 << 20
+KERNEL_VMEM = 47 << 20
 CORES = 2
 SEND_R, SEND_L, FROM_L, FROM_R = range(4)
 E_RS, E_AG, P_AG, D_RS, U_AG = range(5)
@@ -53,7 +53,7 @@
     n_tp, tok, hg, eg, fg, og, hid_h, emb_h, head_h, pw_h, wg_h, wu_h, wd_h,
     pu, zst, lse,
     big, hid, land, ebuf, pbuf, pw, wg, wu, wd, erl, err, drl, drr,
-    onehot, ids_ref, mst, sst, stats,
+    onehot, obuf, ids_ref, mst, sst, stats,
     ring, xsend, xrecv, wsend, wrecv, ssend, srecv, lsem, bsem, hsem,
 ):
     groups, half_rows, dim = hid.shape
@@ -71,7 +71,6 @@
     width = wg.shape[1]
     nbuf = onehot.at[pl.ds(0, half_rows), pl.ds(0, dim)]
     abuf = onehot.at[pl.ds(half_rows, half_rows), pl.ds(0, width)]
-    obuf = onehot.at[:, pl.ds(0, dim)]
     q = big.shape[1]
     n_vq, n_dq = vocab // q, dim // q
 
@@ -91,9 +90,10 @@
             device_id={"tp": dev}, device_id_type=pl.DeviceIdType.MESH,
         )
 
-    def emb_copy(i, j):
+    def emb_copy(i, j, h):
+        w = q // 2
         return pltpu.make_async_copy(
-            emb_h.at[pl.ds(i * q, q), pl.ds(j * q, q)], big.at[j * n_vq + i], bsem.at[j * n_vq + i])
+            emb_h.at[pl.ds(i * q, q), pl.ds(j * q + h * w, w)], big.at[j * n_vq + i, :, pl.ds(h * w, w)], bsem.at[(j * n_vq + i) * 2 + h])
 
     def head_copy(i, j):
         return pltpu.make_async_copy(
@@ -120,8 +120,9 @@
     for d in range(1, n_tp):
         pl.semaphore_signal(barrier, inc=1, device_id={"tp": lax.rem(me + d, n_tp)}, device_id_type=pl.DeviceIdType.MESH)
     for j in range(n_dq):
-        for i in range(n_vq):
-            emb_copy(i, j).start()
+        for h in range(2):
+            for i in range(n_vq):
+                emb_copy(i, j, h).start()
 
     def e_blk(g, o, h):
         cols = pl.ds(0, dim) if h is None else pl.ds(h * hcol, hcol)
@@ -227,21 +228,17 @@
             here = (lane + j * lanes).astype(F32)
             onehot[:, aligned(j, lanes)] = jnp.where(ids_ref[...] == here, 1.0, 0.0).astype(BF16)
 
-    def pick_cols(g, j):
-        tn = tile_of(q, 1024)
-
-        @pl.loop(0, q // tn)
-        def _(t):
-            table = big[j * n_vq:(j + 1) * n_vq, :, aligned(t, tn)].reshape(vocab, tn)
-            acc = jnp.dot(onehot[...], table, preferred_element_type=F32)
-            pu[g, :, pl.ds(pl.multiple_of(j * q + t * tn, tn), tn)] = acc.astype(BF16)
+    def pick_cols(g, j, tn, t=0):
+        table = big[j * n_vq:(j + 1) * n_vq, :, t * tn:(t + 1) * tn].reshape(vocab, tn)
+        acc = jnp.dot(onehot[...], table, preferred_element_type=F32)
+        pu[g, :, j * q + t * tn:j * q + (t + 1) * tn] = acc.astype(BF16)
 
     def picks(g, j):
         @pl.when(g > 0)
         def _():
             if j == 0:
                 one_hot(g)
-            pick_cols(g, j)
+            pick_cols(g, j, q)
             if j == n_dq - 1:
                 pick_swap(g).start()
 
@@ -337,10 +334,22 @@
         pu[g, pl.ds(pl.multiple_of(k * half_rows + z * blk, blk), blk), :] = total.astype(BF16)
         ag_send(U_AG, u_blk, g, 1)
 
+    def o_half(g, c):
+        slot = lax.rem(g, 2)
+
+        def at(r):
+            return pl.ds(pl.multiple_of(c * half_rows + r.start, 16), r.size)
+
+        def put(r, v):
+            obuf[slot, at(r), :] = v
+
+        norm_into(lambda r: pu[g, at(r), :], put, og, half_rows)
+
     def u_done(g):
         for cp in ag_wait(U_AG, u_blk, g, hops):
             cp.wait_recv()
         u_swap(g, k).start()
+        o_half(g, k)
 
     head_tn = tile_of(q, 512)
     per_piece = q // head_tn
@@ -372,17 +381,14 @@
                     for jj in range(n_vq):
                         head_copy(i, jj).wait()
 
-            def put(r, v):
-                obuf[r, :] = v
-
-            norm_into(lambda r: pu[g, r, :], put, og, rows)
+            o_half(g, other)
 
         for t in range(per_piece):
             tile = j * per_piece + t
             if tile > 0:
                 lane_stats(g, tile - 1)
             weights = big[j * n_dq:(j + 1) * n_dq, :, t * head_tn:(t + 1) * head_tn].reshape(dim, head_tn)
-            acc = jnp.dot(obuf[...], weights, preferred_element_type=F32)
+            acc = jnp.dot(obuf[lax.rem(g, 2)], weights, preferred_element_type=F32)
             zst[g, :, tile * head_tn:(tile + 1) * head_tn] = acc
 
     def row_stats(g):
@@ -430,23 +436,24 @@
     order = []
     for i, pieces in enumerate(stages):
         for p in range(len(pieces)):
-            place = (1.0 if i == last else -1.5 if (i, p) == (0, 0) else -i + p * 1.0, p > 0)
+            place = (1.0 if i == last else -3.5 if (i, p) == (0, 0) else -i + p * 1.0, p > 0)
             order.append((place, i, p))
     order.sort()
 
     one_hot(0)
     for j in range(n_dq):
-        for i in range(n_vq):
-            emb_copy(i, j).wait()
-        if j == n_dq - 1:
-            for c in w_local:
-                c.start()
-
-            @pl.loop(0, groups)
-            def _(g):
-                hid_copy(g).start()
-
-        pick_cols(0, j)
+        for h in range(2):
+            for i in range(n_vq):
+                emb_copy(i, j, h).wait()
+            if (j, h) == (n_dq - 1, 1):
+                for c in w_local:
+                    c.start()
+
+                @pl.loop(0, groups)
+                def _(g):
+                    hid_copy(g).start()
+
+            pick_cols(0, j, q // 2, h)
     pl.semaphore_wait(barrier, n_tp - 1)
     pick_swap(0).start()
     w_local[0].wait()
@@ -560,6 +567,7 @@
             pltpu.VMEM((groups, hops, blk, dim), F32),
             pltpu.VMEM((groups, hops, blk, dim), F32),
             pltpu.VMEM((GROUP_ROWS, vocab), BF16),
+            pltpu.VMEM((2, GROUP_ROWS, dim), BF16),
             pltpu.VMEM((GROUP_ROWS, lanes), F32),
             pltpu.VMEM((GROUP_ROWS, lanes), F32),
             pltpu.VMEM((GROUP_ROWS, lanes), F32),
@@ -572,7 +580,7 @@
             dma((groups, n_tp)),
             dma((groups, n_tp)),
             dma((4 + groups,)),
-            dma((n_big,)),
+            dma((2 * n_big,)),
             dma((n_big,)),
         ],
         compiler_params=pltpu.CompilerParams(

time: 177 us -> 176 us (level)
  no operation moved by 1% of the time
where the time goes in v5:
time: 176 us
  Pallas kernels  175 us (99%)
    pallas_call x1, Pallas kernels, draft_call(): pl.pallas_call(functools.partial(step_kernel, n_tp), out_shape=(pltpu.VME...  169 us
    pallas_call x1, Pallas kernels, finish_call(): pl.pallas_call(finish_kernel, grid=(batch // step,), out_shape=(jax.Shape...  5.97 us

profile of v5, /device:TPU:21, one launch (start us, length us, event | category | flops | bytes accessed | tf_op | source)
XLA Modules:
  0.0 175.8 jit_solution(7988481310100794381)
XLA Ops:
  0.6 169.2 %draft_step.1 = (bf16[4,256,2048]{2,1,0:T(8,128)(2,1)S(1)}, f32[4,256,3072]{2,1,0:T(8,128)S(1)}, f32[4,256,128]{2,1,0:T(8,128)S(1)}) custom-call(s32[8,128]{1,0:T(8,128)} %bitcast.15, f32[1,2048]{1,0:T(1,128)} %bitcast.11, f32[1,2048]{1,0:T(1,128)} %bitcast.12, f32[1,2048]{1,0:T(1,128)} %bitcast.13, f32[1,2048]{1,0:T(1,128)} %bitcast.14, ...), custom_call_target="tpu_custom_call" | custom-call | flops 33285996544 | bytes 73400320 | tf_op jit(solution)/shard_map/draft_step/pallas_call | solution.py:546
  169.8 6.0 %finish.1 = (f32[1024,3072]{1,0:T(8,128)}, bf16[1024,2048]{1,0:T(8,128)(2,1)}) custom-call(f32[1024,3072]{1,0:T(8,128)S(1)} %bitcast.8, f32[1024,128]{1,0:T(8,128)S(1)} %bitcast.10, bf16[1024,2048]{1,0:T(8,128)(2,1)S(1)} %bitcast.9), custom_call_target="tpu_custom_call" | custom-call | tf_op jit(solution)/shard_map/finish/pallas_call | solution.py:517
